TPU v7x, 32 devices: a whole 2x2x4 slice. The times are simulated.
32 devices in a mesh: parts: 2 (over y), samp: 16 (over z, x, core).
Axes of the slice: x: 2, y: 2, z: 4, core: 2. Of those that a mesh axis runs over, the one named last changes fastest.
Arguments:
- expression: bfloat16 [1024, 20480], P(('parts', 'samp')), parts along dimension 0, may hold values from -6 to 6
- current: bfloat16 [1024, 256], P(('parts', 'samp')), parts along dimension 0, may hold values from -6 to 6
- next_packed: int32 [512, 32], P(('parts', 'samp')), parts along dimension 0, may hold values from -2147483648 to 1789569706, as said below
- covariates: float32 [1024, 64], P(('parts', 'samp')), parts along dimension 0, may hold values from -1 to 1
Outputs:
- scores: float32 [40960, 256], P(('parts', 'samp')), parts along dimension 0
- next_block: bfloat16 [1024, 256], P(('parts', 'samp')), parts along dimension 0
There are 2 independent parts, one for each index of `parts`. A program takes and returns all parts, laid end to end along the dimension named above; each array names one. Nothing has to cross between parts.
Inputs may be any that keep to these rules, and one draw needn't show every extreme that they name: Each word holds the dosages (0, 1 or 2) of 16 consecutive samples of one variant, two bits a sample: sample 16 w + j of variant v in bits 2 j and 2 j + 1 of next_packed[v, w], bit 31 being the sign bit of the int32 word.
All inputs are finite; a program needn't handle non-finite values.
Results may differ from a plain program's by a relative error of at most 0.0004.
Values may be sent and summed in bfloat16 or wider, within the bound.
A program may use at most 64 MiB of HBM per device.

v0:
```python
import jax
import jax.numpy as jnp
from jax import lax
from jax.sharding import PartitionSpec as P


def unpack_words(packed_words):
    shifts = 2 * jnp.arange(16, dtype=jnp.int32)
    fields = jnp.bitwise_and(
        lax.shift_right_logical(packed_words[:, :, None], shifts[None, None, :]), 3
    )
    return fields.reshape(packed_words.shape[0], -1).T.astype(jnp.float32)


def over_samples(left, right):
    return lax.dot_general(
        left, right, (((0,), (0,)), ((), ())), preferred_element_type=jnp.float32
    )


def precise_samples(left, right):
    return lax.dot_general(left, right, (((0,), (0,)), ((), ())), precision=lax.Precision.HIGHEST)


def shards(expression, current, next_packed, covariates):
    group_size = lax.axis_size("samp")
    samples_all = expression.shape[0] * group_size
    scale_factor = float(samples_all) ** (-0.5)
    regrouped = lax.all_to_all(expression, "samp", split_axis=1, concat_axis=0, tiled=True)
    scores = (
        over_samples(regrouped, lax.all_gather(current, "samp", axis=0, tiled=True)) * scale_factor
    )
    packed_words = lax.all_to_all(next_packed, "samp", split_axis=1, concat_axis=0, tiled=True)
    dosage = unpack_words(packed_words)
    local_totals = jnp.sum(dosage, axis=0)
    local_proj = precise_samples(covariates, dosage)
    local_covsum = jnp.sum(covariates, axis=0)
    local_squares = jnp.sum(dosage * dosage, axis=0)
    local_gram = precise_samples(covariates, covariates)
    totals, projected, cov_sums, squares, cov_gram = lax.psum(
        (local_totals, local_proj, local_covsum, local_squares, local_gram), "samp"
    )
    average = totals / samples_all
    loading = projected - cov_sums[:, None] * average[None, :]
    leftover = (
        dosage - average[None, :] - jnp.dot(covariates, loading, precision=lax.Precision.HIGHEST)
    )
    mapped = jnp.dot(cov_gram, loading, precision=lax.Precision.HIGHEST)
    sq_norm = (
        squares
        - samples_all * average * average
        - 2.0 * jnp.sum(loading * loading, axis=0)
        + jnp.sum(loading * mapped, axis=0)
    )
    next_block = (leftover * lax.rsqrt(sq_norm / samples_all + 1e-05)[None, :]).astype(jnp.bfloat16)
    return (scores, next_block)


def solution(mesh):
    in_specs = (
        P(("parts", "samp"), None),
        P(("parts", "samp"), None),
        P(("parts", "samp"), None),
        P(("parts", "samp"), None),
    )
    out_specs = (P(("parts", "samp"), None), P(("parts", "samp"), None))
    return jax.shard_map(shards, mesh=mesh, in_specs=in_specs, out_specs=out_specs, check_vma=False)
```

profile of v0, /device:TPU:8, one launch (start us, length us, event | category | flops | bytes accessed | tf_op | source)
XLA Modules:
  0.0 168.2 jit_solution(882091936499760265)
XLA Ops:
  7.2 1.4 copy.12
  8.5 6.3 %all-to-all-start.1 = ((s32[16,16,2]{0,2,1:T(2,128)}), s32[16,16,2]{0,2,1:T(2,128)S(1)}, u32[]{:S(2)}, u32[]{:S(2)}) async-start(s32[16,16,2]{0,2,1:T(2,128)} %bitcast.2), calls=%async_computation.1 | async-start | bytes 32768 | tf_op jit(solution)/shard_map/all_to_all | solution.py:33
  14.8 2.5 %copy.16 = bf16[4,16,8,1280]{3,2,0,1:T(8,128)(2,1)} copy(bf16[4,16,8,1280]{3,2,1,0:T(8,128)(2,1)} %bitcast.37) | data formatting | bytes 2621440 | tf_op jit(solution)/shard_map/all_to_all | solution.py:29
  17.3 2.5 %all-to-all-done.1 = s32[16,16,2]{0,2,1:T(2,128)S(1)} async-done(((s32[16,16,2]{0,2,1:T(2,128)}), s32[16,16,2]{0,2,1:T(2,128)S(1)}, u32[]{:S(2)}, u32[]{:S(2)}) %all-to-all-start.1) | async-done | bytes 2080 | tf_op jit(solution)/shard_map/all_to_all | solution.py:33
  19.8 0.0 copy-start
  19.8 0.0 copy-start.1
  19.8 5.2 %all-to-all-start = ((bf16[32,16,1280]{2,0,1:T(8,128)(2,1)}), bf16[32,16,1280]{2,0,1:T(8,128)(2,1)S(1)}, u32[]{:S(2)}, u32[]{:S(2)}) async-start(bf16[32,16,1280]{2,0,1:T(8,128)(2,1)} %bitcast.36), calls=%async_computation | async-start | bytes 2621440 | tf_op jit(solution)/shard_map/all_to_all | solution.py:29
  25.1 0.0 all-reduce.3.cloned.1.call-start
  25.1 0.1 shift_right_logical.26
  25.2 0.0 copy-done
  25.2 0.0 copy-done.1
  25.2 41.4 %all_gather.3 = bf16[512,256]{1,0:T(8,128)(2,1)S(1)} all-gather(bf16[32,256]{1,0:T(8,128)(2,1)S(1)} %copy-done.1), channel_id=1, replica_groups=mesh['parts'=2,'samp'=16] {'samp'}, dimensions={0}, use_global_device_ids=true | all-gather | bytes 278528 | tf_op jit(solution)/shard_map/all_gather | solution.py:31
  66.6 0.2 fusion.14
  66.9 0.1 shift_right_logical.22
  67.0 0.1 fusion.9
  67.1 0.1 fusion.5
  67.1 0.9 convolution_bitcast_fusion
  68.0 0.0 all-reduce.3.cloned.1.call-update
  68.1 51.9 %all-reduce = (f32[256]{0:T(256)S(1)}, f32[64]{0:T(128)S(1)}, f32[64,64]{1,0:T(8,128)S(1)}, f32[256]{0:T(256)S(1)}) all-reduce(f32[256]{0:T(256)S(1)} %get-tuple-element.3, f32[64]{0:T(128)S(1)} %reduce_sum.46, f32[64,64]{1,0:T(8,128)S(1)} %fusion.14, f32[256]{0:T(256)S(1)} %get-tuple-element.2), channel_id=1, replica_groups=mesh['parts'=2,'samp'=16] {'samp'}, use_global_device_ids=true, to_apply=%region_1.0 | all-reduce | flops 4672 | bytes 37376 | tf_op jit(solution)/shard_map/psum | solution.py:40
  120.0 0.1 fusion.7
  120.0 35.9 %all-reduce.3.cloned.1.call-done = f32[64,256]{1,0:T(8,128)} async-done(((f32[64,256]{1,0:T(8,128)}), f32[64,256]{1,0:T(8,128)}) %all-reduce.3.cloned.1.call-update) | async-done | bytes 65552 | tf_op jit(solution)/shard_map/psum | solution.py:40
  156.0 0.9 multiply_reduce_fusion
  156.9 1.1 fusion
  158.0 1.7 %fusion.3 = bf16[32,256]{1,0:T(8,128)(2,1)} fusion(f32[256,32]{0,1:T(8,128)S(1)} %fusion.7, f32[32,64]{1,0:T(8,128)S(1)} %copy-done, f32[64,256]{1,0:T(8,128)} %all-reduce.3.cloned.1.call-done, f32[256]{0:T(256)S(1)} %broadcast_multiply_fusion, f32[64]{0:T(128)S(1)} %get-tuple-element.5, f32[256]{0:T(256)S(1)} %add_rsqrt_fusion), kind=kOutput, calls=%fused_computation.8 | convolution fusion | flops 6348800 | bytes 125184 | tf_op jit(solution)/shard_map/dot_general | solution.py:46
  159.7 0.0 all-to-all-done
  159.7 1.6 convolution_multiply_fusion
  (6 shorter events, 0.0 us)
Async XLA Ops:
  8.5 11.3 %all-to-all-start.1 = ((s32[16,16,2]{0,2,1:T(2,128)}), s32[16,16,2]{0,2,1:T(2,128)S(1)}, u32[]{:S(2)}, u32[]{:S(2)}) async-start(s32[16,16,2]{0,2,1:T(2,128)} %bitcast.2), calls=%async_computation.1 | async-start | bytes 32768 | tf_op jit(solution)/shard_map/all_to_all | solution.py:33
  19.8 5.4 %copy-start = (f32[32,64]{1,0:T(8,128)S(1)}, f32[32,64]{1,0:T(8,128)}, u32[]{:S(2)}) copy-start(f32[32,64]{1,0:T(8,128)} %param.7) | copy-start | bytes 24580
  19.8 5.4 %copy-start.1 = (bf16[32,256]{1,0:T(8,128)(2,1)S(1)}, bf16[32,256]{1,0:T(8,128)(2,1)}, u32[]{:S(2)}) copy-start(bf16[32,256]{1,0:T(8,128)(2,1)} %param.5) | copy-start | bytes 49156
  19.8 139.9 %all-to-all-start = ((bf16[32,16,1280]{2,0,1:T(8,128)(2,1)}), bf16[32,16,1280]{2,0,1:T(8,128)(2,1)S(1)}, u32[]{:S(2)}, u32[]{:S(2)}) async-start(bf16[32,16,1280]{2,0,1:T(8,128)(2,1)} %bitcast.36), calls=%async_computation | async-start | bytes 2621440 | tf_op jit(solution)/shard_map/all_to_all | solution.py:29
  25.1 130.9 %all-reduce.3.cloned.1.call-start = ((), (), s32[]{:S(2)}) async-start(), calls=%async_computation.2 | async-start | bytes 131072 | tf_op jit(solution)/shard_map/psum | solution.py:40
Sparse Core Ops, SparseCore 0:
  68.2 87.7 all-reduce.2
where the time goes:
time: 169 us; the launch traced here: 168 us
  blocking collectives  93.3 us (55%)
  waiting for transfers between devices  38.5 us (23%)
  between operations  14.1 us (8%)
  starting transfers between devices  11.5 us (7%)
  matrix products  5.53 us (3%)
  local copies, waits for them, and re-layouts  4.06 us (2%)
    psum x1, blocking collectives, shards(): lax.psum((local_totals, local_proj, local_covsum, local_squares, local_gr...  51.9 us
    all_gather x1, blocking collectives, shards(): lax.all_gather(current, 'samp', axis=0, tiled=True)  41.4 us
    psum x1, waiting for transfers between devices, shards(): lax.psum((local_totals, local_proj, local_covsum, local_squares, local_gr...  35.9 us
    all_to_all x1, starting transfers between devices, shards(): lax.all_to_all(next_packed, 'samp', split_axis=1, concat_axis=0, tiled=True)  6.27 us
    all_to_all x1, starting transfers between devices, shards(): lax.all_to_all(expression, 'samp', split_axis=1, concat_axis=0, tiled=True)  5.22 us
  transfers between devices with their start and end apart: 3, of which 2 were waited for; matrix products, arithmetic and copies ran while one was open for 5% of the time, Pallas kernels for 0%

commit v1 on v0

--- a/solution.py
+++ b/solution.py
@@ -30,7 +30,12 @@
     scores = (
         over_samples(regrouped, lax.all_gather(current, "samp", axis=0, tiled=True)) * scale_factor
     )
-    packed_words = lax.all_to_all(next_packed, "samp", split_axis=1, concat_axis=0, tiled=True)
+    packed_words = jnp.concatenate(
+        lax.all_to_all(
+            jnp.stack(jnp.split(next_packed, lax.axis_size("samp"), axis=1)), "samp", 0, 0
+        ),
+        axis=0,
+    )
     dosage = unpack_words(packed_words)
     local_totals = jnp.sum(dosage, axis=0)
     local_proj = precise_samples(covariates, dosage)

time: 169 us -> 179 us (1.059)
  local copies, waits for them, and re-layouts: 4.06 us -> 14.3 us
    unnamed x5 -> x19, local copies, waits for them, and re-layouts: 1.38 us -> 8.48 us
    split x0 -> x17, local copies, waits for them, and re-layouts: none -> 2.64 us  [shards(): jnp.split(next_packed, lax.axis_size('samp'), axis=1)]
  transfers between devices with their start and end apart: 3 -> 3, of which waited for: 2 -> 2; matrix products, arithmetic and copies ran while one was open for 5% -> 4% of each run, Pallas kernels for 0% -> 0%
where the time goes in v1:
time: 179 us
  blocking collectives  93.3 us (52%)
  waiting for transfers between devices  38.5 us (22%)
  local copies, waits for them, and re-layouts  14.3 us (8%)
  between operations  14.1 us (8%)
  starting transfers between devices  11.5 us (6%)
  matrix products  5.53 us (3%)
    psum x1, blocking collectives, shards(): lax.psum((local_totals, local_proj, local_covsum, local_squares, local_gr...  51.9 us
    all_gather x1, blocking collectives, shards(): lax.all_gather(current, 'samp', axis=0, tiled=True)  41.4 us
    psum x1, waiting for transfers between devices, shards(): lax.psum((local_totals, local_proj, local_covsum, local_squares, local_gr...  35.9 us
    unnamed x19, local copies, waits for them, and re-layouts  8.48 us
    all_to_all x1, starting transfers between devices, shards(): lax.all_to_all(jnp.stack(jnp.split(next_packed, lax.axis_size('samp'), ax...  6.27 us
    all_to_all x1, starting transfers between devices, shards(): lax.all_to_all(expression, 'samp', split_axis=1, concat_axis=0, tiled=True)  5.22 us
  transfers between devices with their start and end apart: 3, of which 2 were waited for; matrix products, arithmetic and copies ran while one was open for 4% of the time, Pallas kernels for 0%

profile of v1, /device:TPU:8, one launch (start us, length us, event | category | flops | bytes accessed | tf_op | source)
XLA Modules:
  0.0 178.5 jit_solution(13629580522161657270)
XLA Ops:
  7.2 1.4 fusion.14
  8.5 0.1 copy.58
  8.6 0.6 constant_dynamic-update-slice_fusion.15
  9.2 0.1 copy.59
  9.3 0.1 copy.60
  9.4 0.1 copy.61
  9.4 0.1 copy.62
  9.5 0.1 copy.63
  9.6 0.1 copy.64
  9.7 0.1 copy.65
  9.8 0.1 copy.66
  9.8 0.1 copy.67
  9.9 0.1 copy.68
  10.0 0.1 copy.69
  10.1 0.1 copy.70
  10.1 0.1 copy.71
  10.2 0.1 copy.72
  10.4 0.6 constant_dynamic-update-slice_fusion.14
  11.0 0.6 constant_dynamic-update-slice_fusion.13
  11.5 0.6 constant_dynamic-update-slice_fusion.12
  12.1 0.6 constant_dynamic-update-slice_fusion.11
  12.7 0.6 constant_dynamic-update-slice_fusion.10
  13.2 0.6 constant_dynamic-update-slice_fusion.9
  13.8 0.6 constant_dynamic-update-slice_fusion.8
  14.4 0.6 constant_dynamic-update-slice_fusion.7
  14.9 0.6 constant_dynamic-update-slice_fusion.6
  15.5 0.6 constant_dynamic-update-slice_fusion.5
  16.0 0.6 constant_dynamic-update-slice_fusion.4
  16.6 0.6 constant_dynamic-update-slice_fusion.3
  17.2 0.6 constant_dynamic-update-slice_fusion.2
  17.7 0.6 constant_dynamic-update-slice_fusion.1
  18.3 0.6 constant_dynamic-update-slice_fusion
  18.9 6.3 %all-to-all-start.1 = ((s32[16,16,2]{1,2,0:T(2,128)}), s32[16,16,2]{1,2,0:T(2,128)S(1)}, u32[]{:S(2)}, u32[]{:S(2)}) async-start(s32[16,16,2]{1,2,0:T(2,128)} %constant_dynamic-update-slice_fusion), calls=%async_computation.1 | async-start | bytes 32768 | tf_op jit(solution)/shard_map/all_to_all | solution.py:34
  25.1 2.5 %copy.77 = bf16[4,16,8,1280]{3,2,0,1:T(8,128)(2,1)} copy(bf16[4,16,8,1280]{3,2,1,0:T(8,128)(2,1)} %bitcast.67) | data formatting | bytes 2621440 | tf_op jit(solution)/shard_map/all_to_all | solution.py:29
  27.6 2.5 %all-to-all-done.1 = s32[16,16,2]{1,2,0:T(2,128)S(1)} async-done(((s32[16,16,2]{1,2,0:T(2,128)}), s32[16,16,2]{1,2,0:T(2,128)S(1)}, u32[]{:S(2)}, u32[]{:S(2)}) %all-to-all-start.1) | async-done | bytes 2080 | tf_op jit(solution)/shard_map/all_to_all | solution.py:34
  30.2 5.2 %all-to-all-start = ((bf16[32,16,1280]{2,0,1:T(8,128)(2,1)}), bf16[32,16,1280]{2,0,1:T(8,128)(2,1)S(1)}, u32[]{:S(2)}, u32[]{:S(2)}) async-start(bf16[32,16,1280]{2,0,1:T(8,128)(2,1)} %bitcast.66), calls=%async_computation | async-start | bytes 2621440 | tf_op jit(solution)/shard_map/all_to_all | solution.py:29
  35.4 0.1 shift_right_logical.26
  35.5 41.4 %all_gather.3 = bf16[512,256]{1,0:T(8,128)(2,1)S(1)} all-gather(bf16[32,256]{1,0:T(8,128)(2,1)S(1)} %copy-done.1), channel_id=1, replica_groups=mesh['parts'=2,'samp'=16] {'samp'}, dimensions={0}, use_global_device_ids=true | all-gather | bytes 278528 | tf_op jit(solution)/shard_map/all_gather | solution.py:31
  77.0 0.2 fusion.15
  77.2 0.1 shift_right_logical.22
  77.3 0.1 fusion.9
  77.5 0.9 convolution_bitcast_fusion
  78.4 51.9 %all-reduce = (f32[256]{0:T(256)S(1)}, f32[64]{0:T(128)S(1)}, f32[64,64]{1,0:T(8,128)S(1)}, f32[256]{0:T(256)S(1)}) all-reduce(f32[256]{0:T(256)S(1)} %get-tuple-element.3, f32[64]{0:T(128)S(1)} %reduce_sum.46, f32[64,64]{1,0:T(8,128)S(1)} %fusion.15, f32[256]{0:T(256)S(1)} %get-tuple-element.2), channel_id=1, replica_groups=mesh['parts'=2,'samp'=16] {'samp'}, use_global_device_ids=true, to_apply=%region_1.0 | all-reduce | flops 4672 | bytes 37376 | tf_op jit(solution)/shard_map/psum | solution.py:45
  130.4 35.9 %all-reduce.3.cloned.1.call-done = f32[64,256]{1,0:T(8,128)} async-done(((f32[64,256]{1,0:T(8,128)}), f32[64,256]{1,0:T(8,128)}) %all-reduce.3.cloned.1.call-update) | async-done | bytes 65552 | tf_op jit(solution)/shard_map/psum | solution.py:45
  166.3 0.9 multiply_reduce_fusion
  167.2 1.1 fusion
  168.4 1.7 fusion.3
  170.1 1.6 convolution_multiply_fusion
  (16 shorter events, 0.3 us)
Async XLA Ops:
  18.9 11.3 %all-to-all-start.1 = ((s32[16,16,2]{1,2,0:T(2,128)}), s32[16,16,2]{1,2,0:T(2,128)S(1)}, u32[]{:S(2)}, u32[]{:S(2)}) async-start(s32[16,16,2]{1,2,0:T(2,128)} %constant_dynamic-update-slice_fusion), calls=%async_computation.1 | async-start | bytes 32768 | tf_op jit(solution)/shard_map/all_to_all | solution.py:34
  30.2 5.4 %copy-start = (f32[32,64]{1,0:T(8,128)S(1)}, f32[32,64]{1,0:T(8,128)}, u32[]{:S(2)}) copy-start(f32[32,64]{1,0:T(8,128)} %param.7) | copy-start | bytes 24580
  30.2 5.4 %copy-start.1 = (bf16[32,256]{1,0:T(8,128)(2,1)S(1)}, bf16[32,256]{1,0:T(8,128)(2,1)}, u32[]{:S(2)}) copy-start(bf16[32,256]{1,0:T(8,128)(2,1)} %param.5) | copy-start | bytes 49156
  30.2 139.9 %all-to-all-start = ((bf16[32,16,1280]{2,0,1:T(8,128)(2,1)}), bf16[32,16,1280]{2,0,1:T(8,128)(2,1)S(1)}, u32[]{:S(2)}, u32[]{:S(2)}) async-start(bf16[32,16,1280]{2,0,1:T(8,128)(2,1)} %bitcast.66), calls=%async_computation | async-start | bytes 2621440 | tf_op jit(solution)/shard_map/all_to_all | solution.py:29
  35.4 130.9 %all-reduce.3.cloned.1.call-start = ((), (), s32[]{:S(2)}) async-start(), calls=%async_computation.2 | async-start | bytes 131072 | tf_op jit(solution)/shard_map/psum | solution.py:45
Sparse Core Ops, SparseCore 0:
  78.5 87.7 all-reduce.2
